TPU v7x, 32 devices: a whole 2x2x4 slice. The times are simulated.
32 devices in a mesh: dev: 32 (over z, y, x, core).
Axes of the slice: x: 2, y: 2, z: 4, core: 2. Of those that a mesh axis runs over, the one named last changes fastest.
Arguments:
- image_feats: bfloat16 [384, 1152], P('dev'), may hold values from -0.1875 to 0.1875
- text_feats: bfloat16 [384, 1152], P('dev'), may hold values from -0.1875 to 0.1875
- image_head: bfloat16 [1152, 640], replicated, may hold values from -0.1875 to 0.1875
- text_head: bfloat16 [1152, 640], replicated, may hold values from -0.1875 to 0.1875
- log_scale: float32 [], replicated, may hold values from 1.6 to 2.3
- logit_bias: float32 [], replicated, may hold values from -8 to -4
- image_group: int32 [384], P('dev'), may hold values from 0 to 191
- text_group: int32 [384], P('dev'), may hold values from 0 to 191
Outputs:
- loss: float32 [], replicated
- grad_images: bfloat16 [384, 1152], P('dev')
- grad_texts: bfloat16 [384, 1152], P('dev')
- grad_scale: float32 [], replicated
- grad_bias: float32 [], replicated
All inputs are finite; a program needn't handle non-finite values.
Results may differ from a plain program's by a relative error of at most 0.0063.
Values may be sent and summed in bfloat16 or wider, within the bound.
No kernel may reach another device: no remote copies, remote signals or barrier semaphores. Data moves between devices by JAX's collectives and lax.ppermute only.
A program may use at most 128 MiB of HBM per device.

v0:
```python
import jax
import jax.numpy as jnp
from jax import lax
from jax.sharding import PartitionSpec as P

epsilon = 1e-06


def normalize(projected):
    length = jnp.sqrt(jnp.sum(projected * projected, axis=1, keepdims=True) + epsilon)
    return (projected / length, length)


def backward_rows(grad_unit, unit_vec, length, weights):
    inner = jnp.sum(unit_vec * grad_unit, axis=1, keepdims=True)
    grad_proj = ((grad_unit - unit_vec * inner) / length).astype(jnp.bfloat16)
    result = lax.dot_general(
        grad_proj, weights, (((1,), (1,)), ((), ())), preferred_element_type=jnp.float32
    )
    return result.astype(jnp.bfloat16)


def on_device(
    image_feats, text_feats, image_head, text_head, log_scale, logit_bias, image_group, text_group
):
    img_unit, img_length = normalize(
        jnp.dot(image_feats, image_head, preferred_element_type=jnp.float32)
    )
    txt_unit, txt_length = normalize(
        jnp.dot(text_feats, text_head, preferred_element_type=jnp.float32)
    )
    img_emb = img_unit.astype(jnp.bfloat16)
    txt_emb = txt_unit.astype(jnp.bfloat16)
    logit_scale = jnp.exp(log_scale)
    pairs = image_feats.shape[0] * lax.axis_size("dev")
    stacked_emb = jnp.stack([img_emb, txt_emb])
    stacked_ids = jnp.stack([image_group, text_group])
    emb_piece = lax.all_gather(stacked_emb, "dev", axis=1, tiled=True)
    id_piece = lax.all_gather(stacked_ids, "dev", axis=1, tiled=True)
    cap_emb = emb_piece[1]
    cosine = lax.dot_general(
        img_emb, cap_emb, (((1,), (1,)), ((), ())), preferred_element_type=jnp.float32
    )
    label_sign = jnp.where(image_group[:, None] == id_piece[1][None, :], 1.0, -1.0).astype(
        jnp.float32
    )
    margin = label_sign * (logit_scale * cosine + logit_bias)
    slopes = -label_sign * jax.nn.sigmoid(-margin)
    grad_img = logit_scale * jnp.dot(
        slopes.astype(jnp.bfloat16), cap_emb, preferred_element_type=jnp.float32
    )
    added = jnp.stack(
        [jnp.sum(jax.nn.softplus(-margin)), jnp.sum(slopes * cosine), jnp.sum(slopes)]
    )
    caption_side = (grad_img, added)
    img_piece = emb_piece[0]
    cosine = lax.dot_general(
        img_piece, txt_emb, (((1,), (1,)), ((), ())), preferred_element_type=jnp.float32
    )
    label_sign = jnp.where(id_piece[0][:, None] == text_group[None, :], 1.0, -1.0).astype(
        jnp.float32
    )
    margin = label_sign * (logit_scale * cosine + logit_bias)
    slopes = (-label_sign * jax.nn.sigmoid(-margin)).astype(jnp.bfloat16)
    update = lax.dot_general(
        slopes, img_piece, (((0,), (0,)), ((), ())), preferred_element_type=jnp.float32
    )
    grad_txt = logit_scale * update
    grad_img, local_sums = caption_side
    totals = lax.psum(local_sums, "dev")
    loss = totals[0] / pairs
    grad_scale = logit_scale * totals[1] / pairs
    grad_bias = totals[2] / pairs
    grad_images = backward_rows(grad_img, img_unit, img_length, image_head)
    grad_texts = backward_rows(grad_txt, txt_unit, txt_length, text_head)
    return (loss, grad_images, grad_texts, grad_scale, grad_bias)


def solution(mesh):
    placed = (P("dev", None), P("dev", None), P(), P(), P(), P(), P("dev"), P("dev"))
    return jax.shard_map(
        on_device,
        mesh=mesh,
        in_specs=placed,
        out_specs=(P(), P("dev", None), P("dev", None), P(), P()),
        check_vma=False,
    )
```

profile of v0, /device:TPU:14, one launch (start us, length us, event | category | flops | bytes accessed | tf_op | source)
XLA Modules:
  0.0 142.6 jit_solution(6440908995798048725)
XLA Ops:
  0.6 0.0 copy-start
  0.6 0.0 copy-start.2
  0.7 1.9 %multiply_reduce_fusion.3 = (f32[12]{0:T(128)S(1)}, f32[12,640]{1,0:T(8,128)S(1)}) fusion(bf16[12,1152]{1,0:T(8,128)(2,1)} %param.8, bf16[1152,640]{1,0:T(8,128)(2,1)} %param.10), kind=kOutput, calls=%fused_computation.22 | convolution fusion | flops 17710068 | bytes 1532976 | tf_op jit(solution)/shard_map/dot_general | solution.py:27
  2.6 0.0 copy-start.3
  2.6 0.0 copy-done
  2.6 0.0 copy-done.2
  2.6 0.4 multiply_reduce_fusion.2
  3.1 0.0 copy-start.5
  3.1 0.1 convert_bitcast_fusion
  3.2 0.4 copy-done.5
  3.6 0.0 copy-done.3
  3.7 31.5 %all_gather.7 = bf16[2,384,640]{2,0,1:T(2,128)(2,1)S(1)} all-gather(bf16[2,12,640]{2,0,1:T(2,128)(2,1)S(1)} %copy.17), channel_id=1, replica_groups=mesh['dev'=32] {'dev'}, dimensions={1}, use_global_device_ids=true | all-gather | bytes 1013760 | tf_op jit(solution)/shard_map/all_gather | solution.py:38
  35.2 0.0 copy-start.7
  35.2 0.0 copy-start.8
  35.2 1.4 fusion.30
  37.9 0.0 copy-done.7
  37.9 0.0 copy-done.8
  38.0 39.9 %all-gather = s32[32,12,2]{1,2,0:T(2,128)S(1)} all-gather(s32[1,12,2]{1,2,0:T(2,128)S(1)} %add_bitcast_fusion), channel_id=1, replica_groups=mesh['dev'=32] {'dev'}, dimensions={0}, use_global_device_ids=true | all-gather | bytes 3168 | tf_op jit(solution)/shard_map/all_gather | solution.py:39
  77.8 0.7 reshape.32
  78.5 0.0 copy-start.6
  78.5 0.8 slice_reduce_fusion
  79.3 0.0 copy-start.4
  79.3 0.0 copy-start.9
  79.3 2.0 %multiply_reduce_fusion = (f32[12]{0:T(128)S(1)}, f32[12,640]{1,0:T(8,128)}) fusion(f32[12,640]{1,0:T(8,128)S(1)} %get-tuple-element.16, f32[12]{0:T(128)} %copy-done.5, bf16[1,384,640]{2,0,1:T(2,128)(2,1)S(1)} %get-tuple-element.10, f32[]{:T(128)S(6)} %copy.37, f32[]{:T(128)S(6)} %exp.13, s32[384]{0:T(512)S(1)} %get-tuple-element.8, s32[12]{0:T(128)} %param.15), kind=kOutput, calls=%fused_computation.18 | convolution fusion | flops 11888628 | bytes 554648 | tf_op jit(solution)/shard_map/dot_general | solution.py:65
  81.3 0.0 copy-done.6
  81.3 0.0 copy-start.1
  81.3 2.0 %convolution_convert_fusion = bf16[12,1152]{1,0:T(8,128)(2,1)} fusion(bf16[1152,640]{1,0:T(8,128)(2,1)S(1)} %copy-done, f32[12,640]{1,0:T(8,128)} %get-tuple-element.23, f32[12]{0:T(128)S(1)} %get-tuple-element.22, f32[12]{0:T(128)S(1)} %copy-done.6, f32[12,640]{1,0:T(8,128)S(1)} %get-tuple-element.16), kind=kOutput, calls=%fused_computation | convolution fusion | flops 17746944 | bytes 1563744 | tf_op jit(solution)/shard_map/dot_general | solution.py:17
  83.3 0.0 copy-done.4
  83.3 0.0 copy-done.9
  83.3 0.9 fusion.11
  84.3 0.3 multiply_reduce_fusion.1
  84.6 0.0 copy-done.1
  84.6 1.2 convolution_convert_fusion.1
  85.8 2.0 %pad_maximum_fusion.1 = f32[3]{0:T(128)S(1)} fusion(f32[1]{0:T(128)} %bitcast.10, f32[1]{0:T(128)} %bitcast.9, f32[1]{0:T(128)} %bitcast.8), kind=kLoop, calls=%fused_computation.51 | loop fusion | flops 6 | bytes 24 | tf_op jit(solution)/shard_map/stack | solution.py:52
  87.8 48.9 %psum.7 = f32[3]{0:T(128)S(1)} all-reduce(f32[3]{0:T(128)S(1)} %pad_maximum_fusion.1), channel_id=1, replica_groups=mesh['dev'=32] {'dev'}, use_global_device_ids=true, to_apply=%region_5.6 | all-reduce | flops 3 | bytes 24 | tf_op jit(solution)/shard_map/psum | solution.py:70
  136.7 0.6 fusion.31
  (6 shorter events, 0.1 us)
Async XLA Ops:
  0.6 2.0 %copy-start = (bf16[1152,640]{1,0:T(8,128)(2,1)S(1)}, bf16[1152,640]{1,0:T(8,128)(2,1)}, u32[]{:S(2)}) copy-start(bf16[1152,640]{1,0:T(8,128)(2,1)} %param.11) | copy-start | bytes 4423684
  0.6 2.0 %copy-start.2 = (bf16[12,1152]{1,0:T(8,128)(2,1)S(1)}, bf16[12,1152]{1,0:T(8,128)(2,1)}, u32[]{:S(2)}) copy-start(bf16[12,1152]{1,0:T(8,128)(2,1)} %param.9) | copy-start | bytes 82948
  2.6 1.0 copy-start.3
  3.1 0.5 copy-start.5
  35.2 2.7 %copy-start.7 = (s32[12]{0:T(128)S(1)}, s32[12]{0:T(128)}, u32[]{:S(2)}) copy-start(s32[12]{0:T(128)} %param.15) | copy-start | bytes 148
  35.2 2.7 %copy-start.8 = (s32[12]{0:T(128)S(1)}, s32[12]{0:T(128)}, u32[]{:S(2)}) copy-start(s32[12]{0:T(128)} %param.14) | copy-start | bytes 148
  78.5 2.8 %copy-start.6 = (f32[12]{0:T(128)S(1)}, f32[12]{0:T(128)}, u32[]{:S(2)}) copy-start(f32[12]{0:T(128)} %copy-done.5) | copy-start | bytes 148
  79.3 4.0 %copy-start.4 = (f32[12]{0:T(128)S(1)}, f32[12]{0:T(128)}, u32[]{:S(2)}) copy-start(f32[12]{0:T(128)} %copy-done.3) | copy-start | bytes 148
  79.3 4.0 %copy-start.9 = (s32[12]{0:T(128)S(1)}, s32[12]{0:T(128)}, u32[]{:S(2)}) copy-start(s32[12]{0:T(128)} %param.14) | copy-start | bytes 148
  81.3 3.3 %copy-start.1 = (bf16[1152,640]{1,0:T(8,128)(2,1)S(1)}, bf16[1152,640]{1,0:T(8,128)(2,1)}, u32[]{:S(2)}) copy-start(bf16[1152,640]{1,0:T(8,128)(2,1)} %param.10) | copy-start | bytes 4423684
where the time goes:
time: 143 us
  blocking collectives  120 us (84%)
  matrix products  8.77 us (6%)
  between operations  7.46 us (5%)
  local copies, waits for them, and re-layouts  3.95 us (3%)
  other arithmetic  2.13 us (1%)
    psum x1, blocking collectives, on_device(): totals = lax.psum(local_sums, 'dev')  48.9 us
    all_gather x1, blocking collectives, on_device(): id_piece = lax.all_gather(stacked_ids, 'dev', axis=1, tiled=True)  39.9 us
    all_gather x1, blocking collectives, on_device(): emb_piece = lax.all_gather(stacked_emb, 'dev', axis=1, tiled=True)  31.5 us
    dot_general x2, matrix products, backward_rows(): lax.dot_general(grad_proj, weights, (((1,), (1,)), ((), ())), preferred_e...  3.2 us

commit v1 on v0

--- a/solution.py
+++ b/solution.py
@@ -67,7 +67,9 @@
     )
     grad_txt = logit_scale * update
     grad_img, local_sums = caption_side
-    totals = lax.psum(local_sums, "dev")
+    totals = local_sums
+    for hop in (1, 2, 4, 8, 16):
+        totals = totals + lax.ppermute(totals, "dev", [(dev, dev ^ hop) for dev in range(32)])
     loss = totals[0] / pairs
     grad_scale = logit_scale * totals[1] / pairs
     grad_bias = totals[2] / pairs

time: 143 us -> 123 us (0.86)
  the two profiles are of different devices: /device:TPU:14 before, /device:TPU:0 now
where the time goes in v1:
time: 123 us
  blocking collectives  82.8 us (67%)
  waiting for transfers between devices  13.5 us (11%)
  matrix products  8.16 us (7%)
  between operations  7.44 us (6%)
  other arithmetic  6.18 us (5%)
  local copies, waits for them, and re-layouts  2.94 us (2%)
  starting transfers between devices  2.05 us (2%)
    all_gather x1, blocking collectives, on_device(): emb_piece = lax.all_gather(stacked_emb, 'dev', axis=1, tiled=True)  46 us
    all_gather x1, blocking collectives, on_device(): id_piece = lax.all_gather(stacked_ids, 'dev', axis=1, tiled=True)  36.7 us
    ppermute x5, waiting for transfers between devices, on_device(): lax.ppermute(totals, 'dev', [(dev, dev ^ hop) for dev in range(32)])  13.5 us
    add x5, other arithmetic, on_device(): totals + lax.ppermute(totals, 'dev', [(dev, dev ^ hop) for dev in range(3...  4.04 us
  transfers between devices with their start and end apart: 5, of which 4 were waited for; matrix products, arithmetic and copies ran while one was open for 4% of the time, Pallas kernels for 0%

profile of v1, /device:TPU:0, one launch (start us, length us, event | category | flops | bytes accessed | tf_op | source)
XLA Modules:
  0.0 123.0 jit_solution(8556047229400768515)
XLA Ops:
  0.6 0.0 copy-start
  0.6 0.0 copy-start.2
  0.7 1.9 %multiply_reduce_fusion.3 = (f32[12]{0:T(128)S(1)}, f32[12,640]{1,0:T(8,128)S(1)}) fusion(bf16[12,1152]{1,0:T(8,128)(2,1)} %param.8, bf16[1152,640]{1,0:T(8,128)(2,1)} %param.10), kind=kOutput, calls=%fused_computation.22 | convolution fusion | flops 17710068 | bytes 1532976 | tf_op jit(solution)/shard_map/dot_general | solution.py:27
  2.6 0.0 copy-done
  2.6 0.0 copy-done.2
  2.6 0.4 multiply_reduce_fusion.2
  3.1 0.1 convert_bitcast_fusion
  3.2 46.0 %all_gather.7 = bf16[2,384,640]{2,0,1:T(2,128)(2,1)S(1)} all-gather(bf16[2,12,640]{2,0,1:T(2,128)(2,1)S(1)} %copy.17), channel_id=1, replica_groups=mesh['dev'=32] {'dev'}, dimensions={1}, use_global_device_ids=true | all-gather | bytes 1013760 | tf_op jit(solution)/shard_map/all_gather | solution.py:38
  49.2 0.0 copy-start.3
  49.2 0.0 copy-start.4
  49.2 2.2 %fusion.30 = (bf16[1,384,640]{2,0,1:T(2,128)(2,1)}, bf16[1,384,640]{2,0,1:T(2,128)(2,1)S(1)}) fusion(bf16[2,384,640]{2,0,1:T(2,128)(2,1)S(1)} %all_gather.7), kind=kLoop, calls=%fused_computation.57 | loop fusion | bytes 1966080 | tf_op jit(solution)/shard_map/slice | solution.py:56
  52.7 0.0 copy-done.3
  52.8 0.0 copy-done.4
  52.8 36.7 %all-gather = s32[32,12,2]{1,2,0:T(2,128)S(1)} all-gather(s32[1,12,2]{1,2,0:T(2,128)S(1)} %add_bitcast_fusion), channel_id=1, replica_groups=mesh['dev'=32] {'dev'}, dimensions={0}, use_global_device_ids=true | all-gather | bytes 3168 | tf_op jit(solution)/shard_map/all_gather | solution.py:39
  89.5 0.1 reshape.32
  89.6 0.9 fusion.11
  90.6 2.0 %pad_maximum_fusion.1 = f32[3]{0:T(128)S(1)} fusion(f32[1]{0:T(128)} %bitcast.10, f32[1]{0:T(128)} %bitcast.9, f32[1]{0:T(128)} %bitcast.8), kind=kLoop, calls=%fused_computation.51 | loop fusion | flops 6 | bytes 24 | tf_op jit(solution)/shard_map/stack | solution.py:52
  92.6 0.3 collective-permute-start
  92.9 0.3 multiply_reduce_fusion.1
  93.3 0.0 copy-start.1
  93.3 2.2 %multiply_reduce_fusion = (f32[12]{0:T(128)S(1)}, f32[12,640]{1,0:T(8,128)S(1)}) fusion(f32[12,640]{1,0:T(8,128)S(1)} %get-tuple-element.16, f32[12]{0:T(128)S(1)} %add_sqrt_fusion, bf16[1,384,640]{2,0,1:T(2,128)(2,1)} %get-tuple-element.10, f32[]{:T(128)S(6)} %copy.37, f32[]{:T(128)S(6)} %exp.13, s32[384]{0:T(512)S(1)} %get-tuple-element.8, ...), kind=kOutput, calls=%fused_computation.18 | convolution fusion | flops 11888628 | bytes 554648 | tf_op jit(solution)/shard_map/dot_general | solution.py:65
  95.5 1.2 convolution_convert_fusion
  96.7 0.0 copy-done.1
  96.7 1.2 convolution_convert_fusion.1
  97.8 0.0 collective-permute-done
  97.8 2.0 %fusion.40 = f32[3]{0:T(128)S(1)} fusion(f32[3]{0:T(128)S(1)} %collective-permute-done, f32[1]{0:T(128)} %bitcast.10, f32[1]{0:T(128)} %bitcast.9, f32[1]{0:T(128)} %bitcast.8), kind=kLoop, calls=%fused_computation.59 | loop fusion | flops 9 | bytes 36 | tf_op jit(solution)/shard_map/add | solution.py:72
  99.9 1.7 %collective-permute-start.1 = (f32[3]{0:T(128)S(1)}, f32[3]{0:T(128)S(1)}, u32[]{:S(2)}, u32[]{:S(2)}) collective-permute-start(f32[3]{0:T(128)S(1)} %fusion.40), channel_id=1, source_target_pairs={{0,2},{1,3},{2,0},{3,1},{4,6},{5,7},{6,4},{7,5},{8,10},{9,11},{10,... | collective-permute-start | bytes 44 | tf_op jit(solution)/shard_map/ppermute | solution.py:72
  101.5 1.9 %collective-permute-done.1 = f32[3]{0:T(128)S(1)} collective-permute-done((f32[3]{0:T(128)S(1)}, f32[3]{0:T(128)S(1)}, u32[]{:S(2)}, u32[]{:S(2)}) %collective-permute-start.1) | collective-permute-done | bytes 44 | tf_op jit(solution)/shard_map/ppermute | solution.py:72
  103.4 2.0 %fusion.41 = f32[3]{0:T(128)S(1)} fusion(f32[3]{0:T(128)S(1)} %collective-permute-done.1, f32[3]{0:T(128)S(1)} %collective-permute-done, f32[1]{0:T(128)} %bitcast.10, f32[1]{0:T(128)} %bitcast.9, f32[1]{0:T(128)} %bitcast.8), kind=kLoop, calls=%fused_computation.60 | loop fusion | flops 12 | bytes 48 | tf_op jit(solution)/shard_map/add | solution.py:72
  105.5 0.0 collective-permute-start.2
  105.5 3.6 %collective-permute-done.2 = f32[3]{0:T(128)S(1)} collective-permute-done((f32[3]{0:T(128)S(1)}, f32[3]{0:T(128)S(1)}, u32[]{:S(2)}, u32[]{:S(2)}) %collective-permute-start.2) | collective-permute-done | bytes 44 | tf_op jit(solution)/shard_map/ppermute | solution.py:72
  109.0 0.0 collective-permute-start.3
  109.0 3.6 %collective-permute-done.3 = f32[3]{0:T(128)S(1)} collective-permute-done((f32[3]{0:T(128)S(1)}, f32[3]{0:T(128)S(1)}, u32[]{:S(2)}, u32[]{:S(2)}) %collective-permute-start.3) | collective-permute-done | bytes 44 | tf_op jit(solution)/shard_map/ppermute | solution.py:72
  112.6 0.0 collective-permute-start.4
  112.6 4.5 %collective-permute-done.4 = f32[3]{0:T(128)S(1)} collective-permute-done((f32[3]{0:T(128)S(1)}, f32[3]{0:T(128)S(1)}, u32[]{:S(2)}, u32[]{:S(2)}) %collective-permute-start.4) | collective-permute-done | bytes 44 | tf_op jit(solution)/shard_map/ppermute | solution.py:72
  117.1 0.6 fusion.31
  (10 shorter events, 0.1 us)
Async XLA Ops:
  0.6 2.0 %copy-start = (bf16[1152,640]{1,0:T(8,128)(2,1)S(1)}, bf16[1152,640]{1,0:T(8,128)(2,1)}, u32[]{:S(2)}) copy-start(bf16[1152,640]{1,0:T(8,128)(2,1)} %param.11) | copy-start | bytes 4423684
  0.6 2.0 %copy-start.2 = (bf16[12,1152]{1,0:T(8,128)(2,1)S(1)}, bf16[12,1152]{1,0:T(8,128)(2,1)}, u32[]{:S(2)}) copy-start(bf16[12,1152]{1,0:T(8,128)(2,1)} %param.9) | copy-start | bytes 82948
  49.2 3.5 %copy-start.3 = (s32[12]{0:T(128)S(1)}, s32[12]{0:T(128)}, u32[]{:S(2)}) copy-start(s32[12]{0:T(128)} %param.14) | copy-start | bytes 148
  49.2 3.5 %copy-start.4 = (s32[12]{0:T(128)S(1)}, s32[12]{0:T(128)}, u32[]{:S(2)}) copy-start(s32[12]{0:T(128)} %param.15) | copy-start | bytes 148
  92.6 5.3 %collective-permute-start = (f32[3]{0:T(128)S(1)}, f32[3]{0:T(128)S(1)}, u32[]{:S(2)}, u32[]{:S(2)}) collective-permute-start(f32[3]{0:T(128)S(1)} %pad_maximum_fusion.1), channel_id=1, source_target_pairs={{0,1},{1,0},{2,3},{3,2},{4,5},{5,4},{6,7},{7,6},{8,9},{9,8},{10,11... | collective-permute-start | bytes 44 | tf_op jit(solution)/shard_map/ppermute | solution.py:72
  93.3 3.4 %copy-start.1 = (bf16[1152,640]{1,0:T(8,128)(2,1)S(1)}, bf16[1152,640]{1,0:T(8,128)(2,1)}, u32[]{:S(2)}) copy-start(bf16[1152,640]{1,0:T(8,128)(2,1)} %param.10) | copy-start | bytes 4423684
  99.9 3.6 %collective-permute-start.1 = (f32[3]{0:T(128)S(1)}, f32[3]{0:T(128)S(1)}, u32[]{:S(2)}, u32[]{:S(2)}) collective-permute-start(f32[3]{0:T(128)S(1)} %fusion.40), channel_id=1, source_target_pairs={{0,2},{1,3},{2,0},{3,1},{4,6},{5,7},{6,4},{7,5},{8,10},{9,11},{10,... | collective-permute-start | bytes 44 | tf_op jit(solution)/shard_map/ppermute | solution.py:72
  105.5 3.6 %collective-permute-start.2 = (f32[3]{0:T(128)S(1)}, f32[3]{0:T(128)S(1)}, u32[]{:S(2)}, u32[]{:S(2)}) collective-permute-start(f32[3]{0:T(128)S(1)} %fusion.41), channel_id=1, source_target_pairs={{0,4},{1,5},{2,6},{3,7},{4,0},{5,1},{6,2},{7,3},{8,12},{9,13},{10,... | collective-permute-start | bytes 44 | tf_op jit(solution)/shard_map/ppermute | solution.py:72
  109.0 3.6 %collective-permute-start.3 = (f32[3]{0:T(128)S(1)}, f32[3]{0:T(128)S(1)}, u32[]{:S(2)}, u32[]{:S(2)}) collective-permute-start(f32[3]{0:T(128)S(1)} %add.61), channel_id=1, source_target_pairs={{0,8},{1,9},{2,10},{3,11},{4,12},{5,13},{6,14},{7,15},{8,0},{9,1},... | collective-permute-start | bytes 44 | tf_op jit(solution)/shard_map/ppermute | solution.py:72
  112.6 4.5 %collective-permute-start.4 = (f32[3]{0:T(128)S(1)}, f32[3]{0:T(128)S(1)}, u32[]{:S(2)}, u32[]{:S(2)}) collective-permute-start(f32[3]{0:T(128)S(1)} %add.62), channel_id=1, source_target_pairs={{0,16},{1,17},{2,18},{3,19},{4,20},{5,21},{6,22},{7,23},{8,24},{9,... | collective-permute-start | bytes 44 | tf_op jit(solution)/shard_map/ppermute | solution.py:72
